TPU v7x, 128 devices: a whole 4x4x4 slice. The times are simulated.
128 devices in a mesh: tm: 32 (over y, x, core), grp: 4 (over z).
Axes of the slice: x: 4, y: 4, z: 4, core: 2. Of those that a mesh axis runs over, the one named last changes fastest.
Arguments:
- series: float32 [524288, 512], P(('tm', 'grp')), may hold values from -6 to 6
- filter_taps: float32 [33], replicated, may hold values from -1 to 1
- sign_flips: int32 [524288], P(('tm', 'grp')), may hold values from -1 to 1, as said below
- samples: int32 [8192], replicated, may hold values from 0 to 524287, as said below
Outputs:
- sketch: float32 [8192, 512], P(('tm', 'grp'))
- r_factor: float32 [512, 512], replicated
Inputs may be any that keep to these rules, and one draw needn't show every extreme that they name: `sign_flips`: each entry is -1 or +1. All distinct; the values of samples modulo 4096 take exactly 4096 distinct values, each by exactly 2 consecutive entries; entries are ordered by their value modulo 4096, then by value.
All inputs are finite; a program needn't handle non-finite values.
Results may differ from a plain program's by a relative error of at most 0.0003.
Values sent between devices are 32-bit elements; how exact they have to be, the bound alone decides.
No kernel may reach another device: no remote copies, remote signals or barrier semaphores. Data moves between devices by JAX's collectives and lax.ppermute only.
A program may use at most 128 MiB of HBM per device.

v0:
```python
import jax
import jax.numpy as jnp
from jax import lax
from jax.sharding import PartitionSpec as P


def with_halo(array, sides, width):
    edges = {}
    for axis, dim in sides:
        size, length = (lax.axis_size(axis), array.shape[dim])
        up = [(i, (i + 1) % size) for i in range(size - 1)]
        last = lax.slice_in_dim(array, length - width, length, axis=dim)
        leading = lax.slice_in_dim(array, 0, width, axis=dim)
        edges[dim] = (
            lax.ppermute(last, axis, up),
            lax.ppermute(leading, axis, [(b, a) for a, b in up]),
        )
    done = []
    for _, dim in sides:
        low, high = edges[dim]
        around = [(width, width) if d in done else (0, 0) for d in range(array.ndim)]
        array = jnp.concatenate([jnp.pad(low, around), array, jnp.pad(high, around)], axis=dim)
        done.append(dim)
    return array


def bit_count(values, width_bits):
    counted = jnp.zeros_like(values)
    for offset in range(width_bits):
        counted = counted + (values >> offset & 1)
    return counted


def hadamard(order):
    row_ids = jnp.arange(order, dtype=jnp.int32)[:, None]
    col_ids = jnp.arange(order, dtype=jnp.int32)[None, :]
    parity = bit_count(row_ids & col_ids, max(order.bit_length(), 1)) & 1
    return (1 - 2 * parity).astype(jnp.float32)


def local_transform(rows_block):
    length, columns = rows_block.shape
    levels = length.bit_length() - 1
    outer = 2 ** ((levels + 1) // 2)
    inner = length // outer
    layered = rows_block.reshape(outer, inner, columns)
    layered = jnp.einsum("ux,xvw->uvw", hadamard(outer), layered, precision=lax.Precision.HIGHEST)
    layered = jnp.einsum("vy,uyw->uvw", hadamard(inner), layered, precision=lax.Precision.HIGHEST)
    return layered.reshape(length, columns)


def on_device(series, filter_taps, sign_flips, samples):
    rows_dev = series.shape[0]
    columns = series.shape[1]
    tap_count = filter_taps.shape[0]
    half_taps = (tap_count - 1) // 2
    devices_all = lax.axis_size("tm") * lax.axis_size("grp")
    total_rows = rows_dev * devices_all
    sample_count = samples.shape[0]
    padded = with_halo(series, ((("tm", "grp"), 0),), half_taps)
    filtered = filter_taps[0] * padded[0:rows_dev]
    for offset in range(1, tap_count):
        filtered = filtered + filter_taps[offset] * padded[offset : offset + rows_dev]
    flipped = filtered * sign_flips.astype(jnp.float32)[:, None]
    mixed = local_transform(flipped)
    position = lax.axis_index("tm") * lax.axis_size("grp") + lax.axis_index("grp")
    row_scale = 1.0 / jnp.sqrt(jnp.float32(total_rows))
    block_rows = sample_count // devices_all
    copies = max(2, sample_count // rows_dev)
    distinct = sample_count // copies
    per_device = distinct // devices_all
    used_positions = samples[::copies] % rows_dev
    outgoing = jnp.take(mixed, used_positions, axis=0)
    incoming = lax.all_to_all(outgoing, ("tm", "grp"), split_axis=0, concat_axis=0, tiled=True)
    stacked = incoming.reshape(devices_all, per_device, columns)
    combined = (
        jnp.einsum("op,pkw->okw", hadamard(devices_all), stacked, precision=lax.Precision.HIGHEST)
        * row_scale
    )
    combined = combined.reshape(devices_all * per_device, columns)
    mine = lax.dynamic_slice_in_dim(samples, position * block_rows, block_rows)
    slot_index = mine // rows_dev * per_device + jnp.arange(block_rows, dtype=jnp.int32) // copies
    sketch = jnp.take(combined, slot_index, axis=0)
    local_gram = lax.dot_general(
        sketch,
        sketch,
        (((0,), (0,)), ((), ())),
        precision=lax.Precision.HIGHEST,
        preferred_element_type=jnp.float32,
    )
    gram = lax.psum(local_gram, ("tm", "grp"))
    lower = jnp.linalg.cholesky(gram / sample_count)
    return (sketch, lower.T)


def solution(mesh):
    return jax.shard_map(
        on_device,
        mesh=mesh,
        in_specs=(P(("tm", "grp"), None), P(), P(("tm", "grp")), P()),
        out_specs=(P(("tm", "grp"), None), P()),
        check_vma=False,
    )
```

profile of v0, /device:TPU:1, one launch (start us, length us, event | category | flops | bytes accessed | tf_op | source)
XLA Modules:
  0.0 597.2 jit_solution(11944672422323260254)
XLA Ops:
  7.9 4.4 collective-permute-start
  12.3 4.6 collective-permute-start.1
  18.3 2.1 fusion.121
  20.4 1.9 fusion.122
  23.7 11.5 %constant_dynamic-update-slice_fusion = (f32[4112,512]{1,0:T(8,128)}, f32[4112,512]{1,0:T(8,128)}) fusion(f32[4112,512]{1,0:T(8,128)} %constant_dynamic-update-slice_fusion.1, f32[4096,512]{1,0:T(8,128)} %param.4), kind=kLoop, calls=%fused_computation.157 | loop fusion | bytes 25165824 | tf_op jit(solution)/shard_map/concatenate | solution.py:22
  35.9 122.7 %fusion.1 = f32[4096,512]{1,0:T(8,128)S(1)} fusion(f32[4112,512]{1,0:T(8,128)} %constant_dynamic-update-slice_fusion.2, f32[4112,512]{1,0:T(8,128)} %get-tuple-element.10, f32[4096,512]{1,0:T(8,128)} %param.4, f32[4096]{0:T(1024)S(1)} %convert_element_type.14, f32[]{:T(128)} %bitcast.34, f32[]{:T(128)} %bitcast.33, f32[]{:T(128)} %bitcast.32, f32[]{:T(128)} %bitcast.31, ...), kind=kLoop, calls=%fused_computation.4 | loop fusion | flops 138412032 | bytes 285229184 | tf_op jit(solution)/shard_map/mul | solution.py:64
  158.6 12.4 %fusion.37 = f32[64,64,512]{2,0,1:T(8,128)S(1)} fusion(f32[64,64,512]{2,1,0:T(8,128)S(1)} %bitcast.75), kind=kOutput, calls=%fused_computation.71 | convolution fusion | flops 1610715136 | bytes 16777216 | tf_op jit(solution)/shard_map/ux,xvw->uvw/dot_general | solution.py:47
  171.0 13.7 %fusion.35 = f32[64,512,64]{1,2,0:T(8,128)} fusion(f32[64,64,512]{2,0,1:T(8,128)S(1)} %fusion.37), kind=kOutput, calls=%fused_computation.69 | convolution fusion | flops 1610715136 | bytes 16777216 | tf_op jit(solution)/shard_map/vy,uyw->uvw/dot_general | solution.py:48
  184.8 21.4 %gather_fusion = f32[4096,512]{1,0:T(8,128)} fusion(f32[4096,512]{1,0:T(8,128)} %bitcast.73, s32[4096]{0:T(1024)S(1)} %broadcast_clamp_fusion), kind=kCustom, calls=%fused_computation | custom fusion | bytes 16793600 | tf_op jit(solution)/shard_map/jit(_take)/gather | solution.py:73
  206.2 5.8 broadcast_select_fusion
  212.0 8.8 %all-to-all-start = ((f32[128,32,512]{2,1,0:T(8,128)}), f32[128,32,512]{2,1,0:T(8,128)}, u32[]{:S(2)}, u32[]{:S(2)}) async-start(f32[128,32,512]{2,1,0:T(8,128)} %broadcast_select_fusion), calls=%async_computation | async-start | bytes 16777216 | tf_op jit(solution)/shard_map/all_to_all | solution.py:74
  221.7 101.7 %all-to-all-done = f32[128,32,512]{2,1,0:T(8,128)} async-done(((f32[128,32,512]{2,1,0:T(8,128)}), f32[128,32,512]{2,1,0:T(8,128)}, u32[]{:S(2)}, u32[]{:S(2)}) %all-to-all-start) | async-done | bytes 8388640 | tf_op jit(solution)/shard_map/all_to_all | solution.py:74
  323.4 17.0 %broadcast_multiply_fusion = f32[128,32,512]{2,0,1:T(8,128)S(1)} fusion(f32[128,32,512]{2,1,0:T(8,128)} %all-to-all-done), kind=kOutput, calls=%fused_computation.73 | convolution fusion | flops 3223781376 | bytes 16777216 | tf_op jit(solution)/shard_map/op,pkw->okw/dot_general | solution.py:77
  340.5 8.1 %copy.18 = f32[128,32,512]{2,1,0:T(8,128)} copy(f32[128,32,512]{2,0,1:T(8,128)S(1)} %broadcast_multiply_fusion) | data formatting | bytes 16777216 | tf_op jit(solution)/shard_map/mul | solution.py:77
  348.5 4.1 gather_fusion.1
  352.7 2.0 fusion.123
  354.8 147.3 %all-reduce.3.cloned.1.call-done = f32[512,512]{0,1:T(8,128)} async-done(((f32[512,512]{0,1:T(8,128)}), f32[512,512]{0,1:T(8,128)}) %all-reduce.3.cloned.1.call-update) | async-done | bytes 1048592 | tf_op jit(solution)/shard_map/psum | solution.py:91
  505.2 11.7 %cholesky.104 = f32[128,128]{1,0:T(8,128)S(1)} custom-call(f32[128,128]{1,0:T(8,128)S(1)} %cholesky.266), custom_call_target="Cholesky" | custom-call | tf_op jit(solution)/shard_map/jit(cholesky)/cholesky | solution.py:92
  517.1 10.0 %custom-call.27 = f32[1,128,128]{1,2,0:T(8,128)S(1)} custom-call(f32[1,128,128]{2,1,0:T(8,128)S(1)} %get-tuple-element.23), custom_call_target="InvertDiagBlocksLowerTriangular" | custom-call | tf_op jit(solution)/shard_map/jit(cholesky)/cholesky | solution.py:92
  527.8 11.7 %cholesky.217 = f32[128,128]{1,0:T(8,128)S(1)} custom-call(f32[128,128]{1,0:T(8,128)S(1)} %cholesky.270), custom_call_target="Cholesky" | custom-call | tf_op jit(solution)/shard_map/jit(cholesky)/cholesky | solution.py:92
  539.5 9.8 %custom-call.28 = f32[1,128,128]{1,2,0:T(8,128)S(1)} custom-call(f32[1,128,128]{2,1,0:T(8,128)S(1)} %get-tuple-element.20), custom_call_target="InvertDiagBlocksLowerTriangular" | custom-call | tf_op jit(solution)/shard_map/jit(cholesky)/cholesky | solution.py:92
  550.0 11.7 %cholesky.238 = f32[128,128]{1,0:T(8,128)S(1)} custom-call(f32[128,128]{1,0:T(8,128)S(1)} %cholesky.275), custom_call_target="Cholesky" | custom-call | tf_op jit(solution)/shard_map/jit(cholesky)/cholesky | solution.py:92
  561.7 10.0 %custom-call.29 = f32[1,128,128]{1,2,0:T(8,128)S(1)} custom-call(f32[1,128,128]{2,1,0:T(8,128)S(1)} %get-tuple-element.17), custom_call_target="InvertDiagBlocksLowerTriangular" | custom-call | tf_op jit(solution)/shard_map/jit(cholesky)/cholesky | solution.py:92
  572.4 11.7 %cholesky.255 = f32[128,128]{1,0:T(8,128)S(1)} custom-call(f32[128,128]{1,0:T(8,128)S(1)} %convolution_subtract_fusion.2), custom_call_target="Cholesky" | custom-call | tf_op jit(solution)/shard_map/jit(cholesky)/cholesky | solution.py:92
  (39 shorter events, 13.8 us)
Async XLA Ops:
  7.9 15.2 %collective-permute-start = (f32[16,512]{1,0:T(8,128)S(1)}, f32[16,512]{1,0:T(8,128)S(1)}, u32[]{:S(2)}, u32[]{:S(2)}) collective-permute-start(f32[16,512]{1,0:T(8,128)S(1)} %get-tuple-element.12), channel_id=1, source_target_pairs={{0,1},{1,2},{2,3},{3,4},{4,5},{5,6},{6,7},{7,8},{8,9},{9,10},{10,1... | collective-permute-start | bytes 98312 | tf_op jit(solution)/shard_map/ppermute | solution.py:15
  12.3 23.0 %collective-permute-start.1 = (f32[16,512]{1,0:T(8,128)S(1)}, f32[16,512]{1,0:T(8,128)S(1)}, u32[]{:S(2)}, u32[]{:S(2)}) collective-permute-start(f32[16,512]{1,0:T(8,128)S(1)} %get-tuple-element.13), channel_id=1, source_target_pairs={{1,0},{2,1},{3,2},{4,3},{5,4},{6,5},{7,6},{8,7},{9,8},{10,9},{11,1... | collective-permute-start | bytes 98312 | tf_op jit(solution)/shard_map/ppermute | solution.py:16
  212.0 111.4 %all-to-all-start = ((f32[128,32,512]{2,1,0:T(8,128)}), f32[128,32,512]{2,1,0:T(8,128)}, u32[]{:S(2)}, u32[]{:S(2)}) async-start(f32[128,32,512]{2,1,0:T(8,128)} %broadcast_select_fusion), calls=%async_computation | async-start | bytes 16777216 | tf_op jit(solution)/shard_map/all_to_all | solution.py:74
  220.8 281.2 %all-reduce.3.cloned.1.call-start = ((), (), s32[]{:S(2)}) async-start(), calls=%async_computation.1 | async-start | bytes 2097152 | tf_op jit(solution)/shard_map/psum | solution.py:91
  352.7 236.1 %copy-start = (f32[64,512]{1,0:T(8,128)}, f32[64,512]{1,0:T(8,128)S(1)}, u32[]{:S(2)}) copy-start(f32[64,512]{1,0:T(8,128)S(1)} %broadcast_select_fusion.1) | copy-start | bytes 393220
Sparse Core Ops, SparseCore 0:
  354.9 147.1 all-reduce.2
where the time goes:
time: 602 us; the launch traced here: 597 us
  waiting for transfers between devices  249 us (41%)
  other arithmetic  212 us (35%)
  local copies, waits for them, and re-layouts  54.3 us (9%)
  matrix products  47.1 us (8%)
  starting transfers between devices  17.8 us (3%)
  between operations  17.1 us (3%)
    psum x1, waiting for transfers between devices, on_device(): gram = lax.psum(local_gram, ('tm', 'grp'))  147 us
    mul x1, other arithmetic, on_device(): flipped = filtered * sign_flips.astype(jnp.float32)[:, None]  123 us
    all_to_all x1, waiting for transfers between devices, on_device(): lax.all_to_all(outgoing, ('tm', 'grp'), split_axis=0, concat_axis=0, tile...  102 us
    another operation x14, other arithmetic, on_device(): lower = jnp.linalg.cholesky(gram / sample_count)  78.9 us
    gather x1, local copies, waits for them, and re-layouts, on_device(): outgoing = jnp.take(mixed, used_positions, axis=0)  21.4 us
    dot_general x1, matrix products, on_device(): jnp.einsum('op,pkw->okw', hadamard(devices_all), stacked, precision=lax.P...  17 us
    dot_general x1, matrix products, local_transform(): jnp.einsum('vy,uyw->uvw', hadamard(inner), layered, precision=lax.Precisi...  13.7 us
    dot_general x1, matrix products, local_transform(): jnp.einsum('ux,xvw->uvw', hadamard(outer), layered, precision=lax.Precisi...  12.4 us
  transfers between devices with their start and end apart: 4, of which 2 were waited for; matrix products, arithmetic and copies ran while one was open for 3% of the time, Pallas kernels for 0%

commit v1 on v0

--- a/solution.py
+++ b/solution.py
@@ -88,7 +88,7 @@
         precision=lax.Precision.HIGHEST,
         preferred_element_type=jnp.float32,
     )
-    gram = lax.psum(local_gram, ("tm", "grp"))
+    gram = lax.psum(lax.psum(local_gram, "grp"), "tm")
     lower = jnp.linalg.cholesky(gram / sample_count)
     return (sketch, lower.T)
 

time: 602 us -> 609 us (1.012)
  waiting for transfers between devices: 249 us -> 256 us
    psum x1 -> x2, waiting for transfers between devices: 147 us -> 154 us  [on_device(): gram = lax.psum(lax.psum(local_gram, 'grp'), 'tm')]
  transfers between devices with their start and end apart: 4 -> 5, of which waited for: 2 -> 3; matrix products, arithmetic and copies ran while one was open for 3% -> 3% of each run, Pallas kernels for 0% -> 0%
where the time goes in v1:
time: 609 us; the launch traced here: 604 us
  waiting for transfers between devices  256 us (42%)
  other arithmetic  212 us (35%)
  local copies, waits for them, and re-layouts  54.3 us (9%)
  matrix products  47.4 us (8%)
  starting transfers between devices  18 us (3%)
  between operations  17.1 us (3%)
    psum x2, waiting for transfers between devices, on_device(): gram = lax.psum(lax.psum(local_gram, 'grp'), 'tm')  154 us
    mul x1, other arithmetic, on_device(): flipped = filtered * sign_flips.astype(jnp.float32)[:, None]  123 us
    all_to_all x1, waiting for transfers between devices, on_device(): lax.all_to_all(outgoing, ('tm', 'grp'), split_axis=0, concat_axis=0, tile...  102 us
    another operation x14, other arithmetic, on_device(): lower = jnp.linalg.cholesky(gram / sample_count)  78.6 us
    gather x1, local copies, waits for them, and re-layouts, on_device(): outgoing = jnp.take(mixed, used_positions, axis=0)  21.4 us
    dot_general x1, matrix products, on_device(): jnp.einsum('op,pkw->okw', hadamard(devices_all), stacked, precision=lax.P...  17.6 us
    dot_general x1, matrix products, local_transform(): jnp.einsum('vy,uyw->uvw', hadamard(inner), layered, precision=lax.Precisi...  13.5 us
    dot_general x1, matrix products, local_transform(): jnp.einsum('ux,xvw->uvw', hadamard(outer), layered, precision=lax.Precisi...  12.4 us
  transfers between devices with their start and end apart: 5, of which 3 were waited for; matrix products, arithmetic and copies ran while one was open for 3% of the time, Pallas kernels for 0%

profile of v1, /device:TPU:1, one launch (start us, length us, event | category | flops | bytes accessed | tf_op | source)
XLA Modules:
  0.0 604.3 jit_solution(6176581096467166493)
XLA Ops:
  7.9 4.4 collective-permute-start
  12.3 4.6 collective-permute-start.1
  18.3 2.1 fusion.121
  23.7 11.5 %constant_dynamic-update-slice_fusion = (f32[4112,512]{1,0:T(8,128)}, f32[4112,512]{1,0:T(8,128)}) fusion(f32[4112,512]{1,0:T(8,128)} %constant_dynamic-update-slice_fusion.1, f32[4096,512]{1,0:T(8,128)} %param.4), kind=kLoop, calls=%fused_computation.157 | loop fusion | bytes 25165824 | tf_op jit(solution)/shard_map/concatenate | solution.py:22
  35.9 122.7 %fusion.1 = f32[4096,512]{1,0:T(8,128)S(1)} fusion(f32[4112,512]{1,0:T(8,128)} %constant_dynamic-update-slice_fusion.2, f32[4112,512]{1,0:T(8,128)} %get-tuple-element.10, f32[4096,512]{1,0:T(8,128)} %param.4, f32[4096]{0:T(1024)S(1)} %convert_element_type.14, f32[]{:T(128)} %bitcast.34, f32[]{:T(128)} %bitcast.33, f32[]{:T(128)} %bitcast.32, f32[]{:T(128)} %bitcast.31, ...), kind=kLoop, calls=%fused_computation.4 | loop fusion | flops 138412032 | bytes 285229184 | tf_op jit(solution)/shard_map/mul | solution.py:64
  158.6 12.4 %fusion.37 = f32[64,64,512]{2,0,1:T(8,128)S(1)} fusion(f32[64,64,512]{2,1,0:T(8,128)S(1)} %bitcast.75), kind=kOutput, calls=%fused_computation.71 | convolution fusion | flops 1610715136 | bytes 16777216 | tf_op jit(solution)/shard_map/ux,xvw->uvw/dot_general | solution.py:47
  171.0 13.5 %fusion.35 = f32[64,512,64]{1,2,0:T(8,128)} fusion(f32[64,64,512]{2,0,1:T(8,128)S(1)} %fusion.37), kind=kOutput, calls=%fused_computation.69 | convolution fusion | flops 1610715136 | bytes 16777216 | tf_op jit(solution)/shard_map/vy,uyw->uvw/dot_general | solution.py:48
  184.6 21.4 %gather_fusion = f32[4096,512]{1,0:T(8,128)} fusion(f32[4096,512]{1,0:T(8,128)} %bitcast.73, s32[4096]{0:T(1024)S(1)} %broadcast_clamp_fusion), kind=kCustom, calls=%fused_computation | custom fusion | bytes 16793600 | tf_op jit(solution)/shard_map/jit(_take)/gather | solution.py:73
  206.0 5.8 broadcast_select_fusion
  211.8 8.8 %all-to-all-start = ((f32[128,32,512]{2,1,0:T(8,128)}), f32[128,32,512]{2,1,0:T(8,128)}, u32[]{:S(2)}, u32[]{:S(2)}) async-start(f32[128,32,512]{2,1,0:T(8,128)} %broadcast_select_fusion), calls=%async_computation | async-start | bytes 16777216 | tf_op jit(solution)/shard_map/all_to_all | solution.py:74
  221.5 101.7 %all-to-all-done = f32[128,32,512]{2,1,0:T(8,128)} async-done(((f32[128,32,512]{2,1,0:T(8,128)}), f32[128,32,512]{2,1,0:T(8,128)}, u32[]{:S(2)}, u32[]{:S(2)}) %all-to-all-start) | async-done | bytes 8388640 | tf_op jit(solution)/shard_map/all_to_all | solution.py:74
  323.2 17.6 %broadcast_multiply_fusion = f32[128,32,512]{2,0,1:T(8,128)S(1)} fusion(f32[128,32,512]{2,1,0:T(8,128)} %all-to-all-done), kind=kOutput, calls=%fused_computation.73 | convolution fusion | flops 3223781376 | bytes 16777216 | tf_op jit(solution)/shard_map/op,pkw->okw/dot_general | solution.py:77
  340.8 8.1 %copy.18 = f32[128,32,512]{2,1,0:T(8,128)} copy(f32[128,32,512]{2,0,1:T(8,128)S(1)} %broadcast_multiply_fusion) | data formatting | bytes 16777216 | tf_op jit(solution)/shard_map/mul | solution.py:77
  348.9 4.1 gather_fusion.1
  353.1 2.0 fusion.123
  355.3 43.2 %all-reduce.4.cloned.1.call-done = f32[512,512]{0,1:T(8,128)} async-done(((f32[512,512]{0,1:T(8,128)}), f32[512,512]{0,1:T(8,128)}) %all-reduce.4.cloned.1.call-update) | async-done | bytes 1048592 | tf_op jit(solution)/shard_map/psum | solution.py:91
  398.5 110.9 %all-reduce.6.cloned.1.call-done = f32[512,512]{0,1:T(8,128)} async-done(((f32[512,512]{0,1:T(8,128)}), f32[512,512]{0,1:T(8,128)}) %all-reduce.6.cloned.1.call-update) | async-done | bytes 1048592 | tf_op jit(solution)/shard_map/psum | solution.py:91
  512.5 11.7 %cholesky.104 = f32[128,128]{1,0:T(8,128)S(1)} custom-call(f32[128,128]{1,0:T(8,128)S(1)} %cholesky.266), custom_call_target="Cholesky" | custom-call | tf_op jit(solution)/shard_map/jit(cholesky)/cholesky | solution.py:92
  524.4 9.8 %custom-call.27 = f32[1,128,128]{1,2,0:T(8,128)S(1)} custom-call(f32[1,128,128]{2,1,0:T(8,128)S(1)} %get-tuple-element.23), custom_call_target="InvertDiagBlocksLowerTriangular" | custom-call | tf_op jit(solution)/shard_map/jit(cholesky)/cholesky | solution.py:92
  534.9 11.7 %cholesky.217 = f32[128,128]{1,0:T(8,128)S(1)} custom-call(f32[128,128]{1,0:T(8,128)S(1)} %cholesky.270), custom_call_target="Cholesky" | custom-call | tf_op jit(solution)/shard_map/jit(cholesky)/cholesky | solution.py:92
  546.6 10.0 %custom-call.28 = f32[1,128,128]{1,2,0:T(8,128)S(1)} custom-call(f32[1,128,128]{2,1,0:T(8,128)S(1)} %get-tuple-element.20), custom_call_target="InvertDiagBlocksLowerTriangular" | custom-call | tf_op jit(solution)/shard_map/jit(cholesky)/cholesky | solution.py:92
  557.3 11.7 %cholesky.238 = f32[128,128]{1,0:T(8,128)S(1)} custom-call(f32[128,128]{1,0:T(8,128)S(1)} %cholesky.275), custom_call_target="Cholesky" | custom-call | tf_op jit(solution)/shard_map/jit(cholesky)/cholesky | solution.py:92
  569.0 9.8 %custom-call.29 = f32[1,128,128]{1,2,0:T(8,128)S(1)} custom-call(f32[1,128,128]{2,1,0:T(8,128)S(1)} %get-tuple-element.17), custom_call_target="InvertDiagBlocksLowerTriangular" | custom-call | tf_op jit(solution)/shard_map/jit(cholesky)/cholesky | solution.py:92
  579.5 11.7 %cholesky.255 = f32[128,128]{1,0:T(8,128)S(1)} custom-call(f32[128,128]{1,0:T(8,128)S(1)} %convolution_subtract_fusion.2), custom_call_target="Cholesky" | custom-call | tf_op jit(solution)/shard_map/jit(cholesky)/cholesky | solution.py:92
  (42 shorter events, 15.9 us)
Async XLA Ops:
  7.9 15.2 %collective-permute-start = (f32[16,512]{1,0:T(8,128)S(1)}, f32[16,512]{1,0:T(8,128)S(1)}, u32[]{:S(2)}, u32[]{:S(2)}) collective-permute-start(f32[16,512]{1,0:T(8,128)S(1)} %get-tuple-element.12), channel_id=1, source_target_pairs={{0,1},{1,2},{2,3},{3,4},{4,5},{5,6},{6,7},{7,8},{8,9},{9,10},{10,1... | collective-permute-start | bytes 98312 | tf_op jit(solution)/shard_map/ppermute | solution.py:15
  12.3 23.0 %collective-permute-start.1 = (f32[16,512]{1,0:T(8,128)S(1)}, f32[16,512]{1,0:T(8,128)S(1)}, u32[]{:S(2)}, u32[]{:S(2)}) collective-permute-start(f32[16,512]{1,0:T(8,128)S(1)} %get-tuple-element.13), channel_id=1, source_target_pairs={{1,0},{2,1},{3,2},{4,3},{5,4},{6,5},{7,6},{8,7},{9,8},{10,9},{11,1... | collective-permute-start | bytes 98312 | tf_op jit(solution)/shard_map/ppermute | solution.py:16
  211.8 111.4 %all-to-all-start = ((f32[128,32,512]{2,1,0:T(8,128)}), f32[128,32,512]{2,1,0:T(8,128)}, u32[]{:S(2)}, u32[]{:S(2)}) async-start(f32[128,32,512]{2,1,0:T(8,128)} %broadcast_select_fusion), calls=%async_computation | async-start | bytes 16777216 | tf_op jit(solution)/shard_map/all_to_all | solution.py:74
  220.7 177.8 %all-reduce.4.cloned.1.call-start = ((), (), s32[]{:S(2)}) async-start(), calls=%async_computation.1 | async-start | bytes 2097152 | tf_op jit(solution)/shard_map/psum | solution.py:91
  353.1 242.8 %copy-start = (f32[64,512]{1,0:T(8,128)}, f32[64,512]{1,0:T(8,128)S(1)}, u32[]{:S(2)}) copy-start(f32[64,512]{1,0:T(8,128)S(1)} %broadcast_select_fusion.1) | copy-start | bytes 393220
  355.1 154.3 %all-reduce.6.cloned.1.call-start = ((), (), s32[]{:S(2)}) async-start(), calls=%async_computation.2 | async-start | bytes 2097152 | tf_op jit(solution)/shard_map/psum | solution.py:91
Sparse Core Ops, SparseCore 0:
  355.2 43.2 all-reduce.3
  401.7 107.6 all-reduce.5
